TPU v7x, 32 devices: a whole 2x2x4 slice. The times are simulated.
32 devices in a mesh: ep: 4 (over z), tp: 8 (over y, x, core).
Axes of the slice: x: 2, y: 2, z: 4, core: 2. Of those that a mesh axis runs over, the one named last changes fastest.
Arguments:
- tokens: bfloat16 [384, 3072], P('ep', 'tp'), may hold values from -6 to 6
- cotangent: bfloat16 [384, 3072], P('ep', 'tp'), may hold values from -6 to 6
- expert_ids: int32 [384, 2], P('ep'), may hold values from 0 to 3, all different within a row; in each aligned block of 96 rows (0 to 95, 96 to 191, ...) at most 80 rows name the same one
- combine_weights: float32 [384, 2], P('ep'), may hold values from 0.1 to 1
- w_gate: bfloat16 [4, 3072, 8192], P('ep', None, 'tp'), may hold values from -0.15625 to 0.15625
- w_up: bfloat16 [4, 3072, 8192], P('ep', None, 'tp'), may hold values from -0.109375 to 0.109375
- w_down: bfloat16 [4, 8192, 3072], P('ep', 'tp'), may hold values from -0.09375 to 0.09375
Outputs:
- mixed: bfloat16 [384, 3072], P('ep', 'tp')
- grad_tokens: bfloat16 [384, 3072], P('ep', 'tp')
- grad_combine: float32 [384, 2], P('ep')
- grad_gate: bfloat16 [4, 3072, 8192], P('ep', 'tp')
- grad_up: bfloat16 [4, 3072, 8192], P('ep', 'tp')
- grad_down: bfloat16 [4, 8192, 3072], P('ep', None, 'tp')
Inputs may be any that keep to these rules, and one draw needn't show every extreme that they name: `expert_ids`: each row names 2 different experts. Among the 96 rows of one index of ep, no expert is named more than 80 times, and in some such blocks one expert is named exactly 80 times.
All inputs are finite; a program needn't handle non-finite values.
Results may differ from a plain program's by a relative error of at most 0.019.
Values may be sent and summed in bfloat16 or wider, within the bound.
A program may use at most 128 MiB of HBM per device.

v0:
```python
import jax
import jax.numpy as jnp
from jax import lax
from jax.sharding import PartitionSpec as P


def silu_parts(gate_pre):
    sigma = jax.nn.sigmoid(gate_pre)
    return (gate_pre * sigma, sigma * (1.0 + gate_pre * (1.0 - sigma)))


def contract_rows(left, right):
    return lax.dot_general(
        left, right, (((0,), (0,)), ((), ())), preferred_element_type=jnp.float32
    )


def contract_cols(left, right):
    return lax.dot_general(
        left, right, (((1,), (1,)), ((), ())), preferred_element_type=jnp.float32
    )


def body(tokens, cotangent, expert_ids, combine_weights, w_gate, w_up, w_down):
    groups = lax.axis_size("ep")
    tok_rows, piece_width = tokens.shape
    chosen = expert_ids.shape[1]
    capacity = tok_rows * chosen * 5 // (3 * groups)
    buffer_rows = groups * capacity
    gate_weight = w_gate[0]
    up_weight = w_up[0]
    down_weight = w_down[0]
    flat_ids = expert_ids.reshape(-1)
    onehot = (flat_ids[:, None] == jnp.arange(groups, dtype=jnp.int32)[None, :]).astype(jnp.int32)
    rank = jnp.sum((jnp.cumsum(onehot, axis=0) - onehot) * onehot, axis=1)
    slot_index = flat_ids * capacity + rank
    places = (jnp.arange(buffer_rows, dtype=jnp.int32)[:, None] == slot_index[None, :]).astype(
        jnp.bfloat16
    )
    placer = jnp.sum(
        places.reshape(buffer_rows, tok_rows, chosen).astype(jnp.float32), axis=2
    ).astype(jnp.bfloat16)
    scaled = (combine_weights[:, :, None] * cotangent[:, None, :].astype(jnp.float32)).astype(
        jnp.bfloat16
    )
    send_grad = jnp.dot(
        places, scaled.reshape(tok_rows * chosen, piece_width), preferred_element_type=jnp.float32
    ).astype(jnp.bfloat16)
    send_rows = jnp.dot(placer, tokens, preferred_element_type=jnp.float32).astype(jnp.bfloat16)
    recv_rows, recv_grad = (
        lax.all_to_all(
            send_rows.reshape(groups, capacity, piece_width),
            "ep",
            split_axis=0,
            concat_axis=0,
            tiled=True,
        ),
        lax.all_to_all(
            send_grad.reshape(groups, capacity, piece_width),
            "ep",
            split_axis=0,
            concat_axis=0,
            tiled=True,
        ),
    )
    recv_rows = recv_rows.reshape(buffer_rows, piece_width)
    piece = lax.all_gather(recv_rows, "tp", axis=1, tiled=True)
    gate_pre = jnp.dot(piece, gate_weight, preferred_element_type=jnp.float32)
    up_pre = jnp.dot(piece, up_weight, preferred_element_type=jnp.float32)
    recv_grad = recv_grad.reshape(buffer_rows, piece_width)
    active, slope = silu_parts(gate_pre)
    hidden = (active * up_pre).astype(jnp.bfloat16)
    partial_value = jnp.dot(hidden, down_weight, preferred_element_type=jnp.float32)
    out_piece = lax.psum_scatter(
        partial_value.astype(jnp.bfloat16), "tp", scatter_dimension=1, tiled=True
    )
    out_back = lax.all_to_all(
        out_piece.reshape(groups, capacity, piece_width),
        "ep",
        split_axis=0,
        concat_axis=0,
        tiled=True,
    ).reshape(buffer_rows, piece_width)
    out_tokens = (
        jnp.take(out_back, slot_index, axis=0)
        .reshape(tok_rows, chosen, piece_width)
        .astype(jnp.float32)
    )
    mixed = jnp.sum(combine_weights[:, :, None] * out_tokens, axis=1).astype(jnp.bfloat16)
    local_products = jnp.sum(cotangent.astype(jnp.float32)[:, None, :] * out_tokens, axis=2)
    grad_combine = lax.psum(local_products, "tp")
    grad_hidden = contract_cols(lax.all_gather(recv_grad, "tp", axis=1, tiled=True), down_weight)
    grad_gate_pre = (grad_hidden * up_pre * slope).astype(jnp.bfloat16)
    grad_up_pre = (grad_hidden * active).astype(jnp.bfloat16)
    input_partial = contract_cols(grad_gate_pre, gate_weight) + contract_cols(
        grad_up_pre, up_weight
    )
    input_piece = lax.psum_scatter(
        input_partial.astype(jnp.bfloat16), "tp", scatter_dimension=1, tiled=True
    )
    input_back = lax.all_to_all(
        input_piece.reshape(groups, capacity, piece_width),
        "ep",
        split_axis=0,
        concat_axis=0,
        tiled=True,
    ).reshape(buffer_rows, piece_width)
    grad_tokens = jnp.sum(
        jnp.take(input_back, slot_index, axis=0)
        .reshape(tok_rows, chosen, piece_width)
        .astype(jnp.float32),
        axis=1,
    ).astype(jnp.bfloat16)
    down_cols_out = contract_rows(
        lax.all_gather(hidden, "tp", axis=1, tiled=True), recv_grad
    ).astype(jnp.bfloat16)
    gate_rows_out = contract_rows(
        recv_rows, lax.all_gather(grad_gate_pre, "tp", axis=1, tiled=True)
    ).astype(jnp.bfloat16)
    up_rows_out = contract_rows(
        recv_rows, lax.all_gather(grad_up_pre, "tp", axis=1, tiled=True)
    ).astype(jnp.bfloat16)
    return (
        mixed,
        grad_tokens,
        grad_combine,
        gate_rows_out[None],
        up_rows_out[None],
        down_cols_out[None],
    )


def solution(mesh):
    placed = (
        P("ep", "tp"),
        P("ep", "tp"),
        P("ep", None),
        P("ep", None),
        P("ep", None, "tp"),
        P("ep", None, "tp"),
        P("ep", "tp", None),
    )
    return jax.shard_map(
        body,
        mesh=mesh,
        in_specs=placed,
        out_specs=(
            P("ep", "tp"),
            P("ep", "tp"),
            P("ep", None),
            P("ep", "tp", None),
            P("ep", "tp", None),
            P("ep", None, "tp"),
        ),
        check_vma=False,
    )
```

profile of v0, /device:TPU:0, one launch (start us, length us, event | category | flops | bytes accessed | tf_op | source)
XLA Modules:
  0.0 345.3 jit_solution(14254782053761471952)
XLA Ops:
  7.2 0.8 copy.43
  8.0 0.1 eq.43
  8.2 1.2 reduce-window.6
  9.9 1.0 mul.83
  10.8 0.2 mul.84
  11.0 0.8 copy.42
  11.8 0.1 mul.81
  11.9 0.3 convolution_convert_fusion.3
  12.3 14.8 %all_to_all.20 = bf16[4,80,384]{2,1,0:T(8,128)(2,1)} all-to-all(bf16[4,80,384]{2,1,0:T(8,128)(2,1)S(1)} %bitcast.73), channel_id=1, replica_groups=mesh['ep'=4,'tp'=8] {'ep'}, dimensions={0} | all-to-all | bytes 491520 | tf_op jit(solution)/shard_map/all_to_all | solution.py:58
  27.3 0.7 multiply_add_fusion.1
  28.2 0.3 convolution_convert_fusion.4
  28.4 10.8 %all_to_all.21 = bf16[4,80,384]{2,1,0:T(8,128)(2,1)} all-to-all(bf16[4,80,384]{2,1,0:T(8,128)(2,1)S(1)} %bitcast.74), channel_id=1, replica_groups=mesh['ep'=4,'tp'=8] {'ep'}, dimensions={0} | all-to-all | bytes 491520 | tf_op jit(solution)/shard_map/all_to_all | solution.py:51
  39.3 14.6 %all-gather.8.cloned.1.call-done = bf16[320,3072]{1,0:T(8,128)(2,1)} async-done(((bf16[320,384]{1,0:T(8,128)(2,1)}), bf16[320,3072]{1,0:T(8,128)(2,1)}) %all-gather.8.cloned.1.call-update) | async-done | bytes 1966096 | tf_op jit(solution)/shard_map/all_gather | solution.py:92
  53.9 5.6 %fusion.3 = f32[320,1024]{1,0:T(8,128)S(1)} fusion(bf16[320,3072]{1,0:T(8,128)(2,1)} %all-gather.8.cloned.1.call-done, bf16[1,1024,3072]{2,1,0:T(8,128)(2,1)} %param.15), kind=kOutput, calls=%fused_computation.8 | convolution fusion | flops 2013265920 | bytes 9568256 | tf_op jit(solution)/shard_map/dot_general | solution.py:19
  59.5 23.8 %all-gather.6.cloned.1.call-done = bf16[320,3072]{1,0:T(8,128)(2,1)} async-done(((bf16[320,384]{1,0:T(8,128)(2,1)}), bf16[320,3072]{1,0:T(8,128)(2,1)}) %all-gather.6.cloned.1.call-update) | async-done | bytes 1966096 | tf_op jit(solution)/shard_map/all_gather | solution.py:67
  83.3 5.7 %fusion.9 = f32[320,1024]{1,0:T(8,128)S(1)} fusion(bf16[320,3072]{1,0:T(8,128)(2,1)} %all-gather.6.cloned.1.call-done, bf16[1,3072,1024]{2,1,0:T(8,128)(2,1)} %param.14), kind=kOutput, calls=%fused_computation.14 | convolution fusion | flops 2013265920 | bytes 9568256 | tf_op jit(solution)/shard_map/dot_general | solution.py:69
  89.0 6.6 %multiply_convert_fusion.1 = (bf16[320,1024]{1,0:T(8,128)(2,1)}, bf16[320,1024]{1,0:T(8,128)(2,1)S(1)}, bf16[320,1024]{1,0:T(8,128)(2,1)}) fusion(f32[320,1024]{1,0:T(8,128)S(1)} %fusion.3, f32[320,1024]{1,0:T(8,128)S(1)} %fusion.9, bf16[320,3072]{1,0:T(8,128)(2,1)S(1)} %copy-done.6, bf16[1,3072,1024]{2,1,0:T(8,128)(2,1)} %param.13), kind=kOutput, calls=%fused_computation.24 | convolution fusion | flops 2018181120 | bytes 12845056 | tf_op jit(solution)/shard_map/dot_general | solution.py:68
  95.6 7.2 %fusion.7 = f32[320,3072]{1,0:T(8,128)} fusion(bf16[320,1024]{1,0:T(8,128)(2,1)S(1)} %get-tuple-element.34, bf16[1,3072,1024]{2,1,0:T(8,128)(2,1)} %param.14), kind=kOutput, calls=%fused_computation.12 | convolution fusion | flops 2013265920 | bytes 10878976 | tf_op jit(solution)/shard_map/dot_general | solution.py:19
  102.8 6.3 %fusion.18 = bf16[320,3072]{1,0:T(8,128)(2,1)S(1)} fusion(f32[320,3072]{1,0:T(8,128)} %fusion.7, bf16[320,1024]{1,0:T(8,128)(2,1)} %get-tuple-element.33, bf16[1,3072,1024]{2,1,0:T(8,128)(2,1)} %param.13), kind=kOutput, calls=%fused_computation.21 | convolution fusion | flops 2015232000 | bytes 12845056 | tf_op jit(solution)/shard_map/dot_general | solution.py:19
  109.1 2.4 copy.51
  111.6 0.2 reduce-scatter.7.cloned.1.call-start
  111.8 5.0 %fusion.21 = bf16[320,3072]{1,0:T(8,128)(2,1)S(1)} fusion(bf16[320,1024]{1,0:T(8,128)(2,1)S(1)} %copy-done.5, bf16[1,1024,3072]{2,1,0:T(8,128)(2,1)} %param.15), kind=kOutput, calls=%fused_computation.22 | convolution fusion | flops 2014248960 | bytes 8912896 | tf_op jit(solution)/shard_map/dot_general | solution.py:73
  116.8 2.4 copy.49
  119.3 0.5 all-gather.10.cloned.1.call-update
  119.9 0.5 all-gather.14.cloned.1.call-update
  120.5 0.7 all-gather.12.cloned.1.call-update
  121.2 32.9 %reduce-scatter.9.cloned.1.call-done = bf16[384,320]{1,0:T(8,128)(2,1)} async-done(((bf16[3072,320]{1,0:T(8,128)(2,1)}), bf16[384,320]{1,0:T(8,128)(2,1)}) %reduce-scatter.9.cloned.1.call-update) | async-done | bytes 245776
  154.1 1.8 copy.52
  155.9 4.6 %all-to-all-start.3 = ((bf16[4,80,384]{2,1,0:T(8,128)(2,1)}), bf16[4,80,384]{2,1,0:T(8,128)(2,1)S(1)}, u32[]{:S(2)}, u32[]{:S(2)}) async-start(bf16[4,80,384]{2,1,0:T(8,128)(2,1)} %bitcast.11), calls=%async_computation.3 | async-start | bytes 491520 | tf_op jit(solution)/shard_map/all_to_all | solution.py:101
  160.5 39.7 %reduce-scatter.7.cloned.1.call-done = bf16[384,320]{1,0:T(8,128)(2,1)} async-done(((bf16[3072,320]{1,0:T(8,128)(2,1)}), bf16[384,320]{1,0:T(8,128)(2,1)}) %reduce-scatter.7.cloned.1.call-update) | async-done | bytes 245776
  200.2 1.8 copy.50
  202.0 4.6 %all-to-all-start.1 = ((bf16[4,80,384]{2,1,0:T(8,128)(2,1)}), bf16[4,80,384]{2,1,0:T(8,128)(2,1)S(1)}, u32[]{:S(2)}, u32[]{:S(2)}) async-start(bf16[4,80,384]{2,1,0:T(8,128)(2,1)} %bitcast.7), calls=%async_computation.1 | async-start | bytes 491520 | tf_op jit(solution)/shard_map/all_to_all | solution.py:77
  206.7 1.0 gather_fusion.1
  207.7 7.3 %all-to-all-done.1 = bf16[4,80,384]{2,1,0:T(8,128)(2,1)S(1)} async-done(((bf16[4,80,384]{2,1,0:T(8,128)(2,1)}), bf16[4,80,384]{2,1,0:T(8,128)(2,1)S(1)}, u32[]{:S(2)}, u32[]{:S(2)}) %all-to-all-start.1) | async-done | bytes 245792 | tf_op jit(solution)/shard_map/all_to_all | solution.py:77
  215.0 1.0 gather_fusion
  216.1 0.2 reshape.99
  216.4 0.2 multiply_reduce_fusion
  216.6 0.1 reduce_sum.61
  216.7 24.0 %psum.7 = f32[96,2]{1,0:T(8,128)S(1)} all-reduce(f32[96,2]{1,0:T(8,128)S(1)} %reduce_sum.61), channel_id=1, replica_groups=mesh['ep'=4,'tp'=8] {'tp'}, use_global_device_ids=true, to_apply=%region_9.11 | all-reduce | flops 192 | bytes 1536 | tf_op jit(solution)/shard_map/psum | solution.py:91
  240.7 0.6 copy.48
  241.3 1.0 reduce_sum.59
  242.3 1.1 multiply_reduce_fusion.1
  243.4 0.8 all-gather.10.cloned.1.call-done
  244.2 8.7 %fusion = bf16[1,384,8192]{2,1,0:T(8,128)(2,1)} fusion(bf16[320,384]{1,0:T(8,128)(2,1)S(1)} %bitcast.69, bf16[320,8192]{1,0:T(8,128)(2,1)} %all-gather.10.cloned.1.call-done), kind=kOutput, calls=%fused_computation.5 | convolution fusion | flops 2016411648 | bytes 11780096 | tf_op jit(solution)/shard_map/dot_general | solution.py:13
  252.8 34.0 %all-gather.14.cloned.1.call-done = bf16[320,8192]{1,0:T(8,128)(2,1)} async-done(((bf16[320,1024]{1,0:T(8,128)(2,1)}), bf16[320,8192]{1,0:T(8,128)(2,1)}) %all-gather.14.cloned.1.call-update) | async-done | bytes 5242896 | tf_op jit(solution)/shard_map/all_gather | solution.py:115
  286.8 9.3 %fusion.2 = bf16[1,8192,384]{2,1,0:T(8,128)(2,1)} fusion(bf16[320,8192]{1,0:T(8,128)(2,1)} %all-gather.14.cloned.1.call-done, bf16[320,384]{1,0:T(8,128)(2,1)S(1)} %bitcast.72), kind=kOutput, calls=%fused_computation.7 | convolution fusion | flops 2016411648 | bytes 11780096 | tf_op jit(solution)/shard_map/dot_general | solution.py:13
  296.2 33.6 %all-gather.12.cloned.1.call-done = bf16[320,8192]{1,0:T(8,128)(2,1)} async-done(((bf16[320,1024]{1,0:T(8,128)(2,1)}), bf16[320,8192]{1,0:T(8,128)(2,1)}) %all-gather.12.cloned.1.call-update) | async-done | bytes 5242896 | tf_op jit(solution)/shard_map/all_gather | solution.py:121
  329.8 8.7 %fusion.1 = bf16[1,384,8192]{2,1,0:T(8,128)(2,1)} fusion(bf16[320,384]{1,0:T(8,128)(2,1)S(1)} %bitcast.70, bf16[320,8192]{1,0:T(8,128)(2,1)} %all-gather.12.cloned.1.call-done), kind=kOutput, calls=%fused_computation.6 | convolution fusion | flops 2016411648 | bytes 11780096 | tf_op jit(solution)/shard_map/dot_general | solution.py:13
  (44 shorter events, 1.3 us)
Async XLA Ops:
  7.2 21.0 %copy-start = (bf16[96,384]{1,0:T(8,128)(2,1)S(1)}, bf16[96,384]{1,0:T(8,128)(2,1)}, u32[]{:S(2)}) copy-start(bf16[96,384]{1,0:T(8,128)(2,1)} %param.9) | copy-start | bytes 221188
  7.2 46.7 %all-gather.8.cloned.1.call-start = ((), (), s32[]{:S(2)}) async-start(), calls=%async_computation.7 | async-start | bytes 2211840 | tf_op jit(solution)/shard_map/all_gather | solution.py:92
  27.1 56.2 %all-gather.6.cloned.1.call-start = ((), (), s32[]{:S(2)}) async-start(), calls=%async_computation.6 | async-start | bytes 2211840 | tf_op jit(solution)/shard_map/all_gather | solution.py:67
  39.2 114.9 %reduce-scatter.9.cloned.1.call-start = ((), (), s32[]{:S(2)}) async-start(), calls=%async_computation.12 | async-start | bytes 2654208
  83.3 5.7 %copy-start.6 = (bf16[320,3072]{1,0:T(8,128)(2,1)S(1)}, bf16[320,3072]{1,0:T(8,128)(2,1)}, u32[]{:S(2)}) copy-start(bf16[320,3072]{1,0:T(8,128)(2,1)} %all-gather.6.cloned.1.call-done) | copy-start | bytes 5898244
  95.6 7.2 %copy-start.4 = (bf16[320,1024]{1,0:T(8,128)(2,1)}, bf16[320,1024]{1,0:T(8,128)(2,1)S(1)}, u32[]{:S(2)}) copy-start(bf16[320,1024]{1,0:T(8,128)(2,1)S(1)} %get-tuple-element.34) | copy-start | bytes 1966084
  109.1 2.7 copy-start.5
  111.6 88.6 %reduce-scatter.7.cloned.1.call-start = ((), (), s32[]{:S(2)}) async-start(), calls=%async_computation.11 | async-start | bytes 2654208
  119.2 124.9 %all-gather.10.cloned.1.call-start = ((), (), s32[]{:S(2)}) async-start(), calls=%async_computation.8 | async-start | bytes 5898240 | tf_op jit(solution)/shard_map/all_gather | solution.py:118
  119.8 167.0 %all-gather.14.cloned.1.call-start = ((), (), s32[]{:S(2)}) async-start(), calls=%async_computation.10 | async-start | bytes 5898240 | tf_op jit(solution)/shard_map/all_gather | solution.py:115
  120.4 209.3 %all-gather.12.cloned.1.call-start = ((), (), s32[]{:S(2)}) async-start(), calls=%async_computation.9 | async-start | bytes 5898240 | tf_op jit(solution)/shard_map/all_gather | solution.py:121
  121.2 123.0 %copy-start.2 = (bf16[4,80,384]{2,1,0:T(8,128)(2,1)S(1)}, bf16[4,80,384]{2,1,0:T(8,128)(2,1)}, u32[]{:S(2)}) copy-start(bf16[4,80,384]{2,1,0:T(8,128)(2,1)} %all_to_all.21) | copy-start | bytes 737284
  155.9 46.2 %all-to-all-start.3 = ((bf16[4,80,384]{2,1,0:T(8,128)(2,1)}), bf16[4,80,384]{2,1,0:T(8,128)(2,1)S(1)}, u32[]{:S(2)}, u32[]{:S(2)}) async-start(bf16[4,80,384]{2,1,0:T(8,128)(2,1)} %bitcast.11), calls=%async_computation.3 | async-start | bytes 491520 | tf_op jit(solution)/shard_map/all_to_all | solution.py:101
  202.0 13.0 %all-to-all-start.1 = ((bf16[4,80,384]{2,1,0:T(8,128)(2,1)}), bf16[4,80,384]{2,1,0:T(8,128)(2,1)S(1)}, u32[]{:S(2)}, u32[]{:S(2)}) async-start(bf16[4,80,384]{2,1,0:T(8,128)(2,1)} %bitcast.7), calls=%async_computation.1 | async-start | bytes 491520 | tf_op jit(solution)/shard_map/all_to_all | solution.py:77
  243.4 43.5 %copy-start.3 = (bf16[4,80,384]{2,1,0:T(8,128)(2,1)S(1)}, bf16[4,80,384]{2,1,0:T(8,128)(2,1)}, u32[]{:S(2)}) copy-start(bf16[4,80,384]{2,1,0:T(8,128)(2,1)} %all_to_all.20) | copy-start | bytes 737284
  286.8 51.6 %copy-start.1 = (bf16[96,384]{1,0:T(8,128)(2,1)S(1)}, bf16[96,384]{1,0:T(8,128)(2,1)}, u32[]{:S(2)}) copy-start(bf16[96,384]{1,0:T(8,128)(2,1)} %param.9) | copy-start | bytes 221188
Sparse Core Ops, SparseCore 0:
  27.2 26.6 all-gather.7
  55.7 27.5 all-gather.5
  111.7 42.3 reduce-scatter.8
  157.8 42.3 reduce-scatter.6
  202.5 41.5 all-gather.9
  245.9 40.8 all-gather.13
  288.7 40.9 all-gather.11
where the time goes:
time: 346 us; the launch traced here: 345 us
  waiting for transfers between devices  189 us (55%)
  matrix products  63.6 us (18%)
  blocking collectives  49.5 us (14%)
  local copies, waits for them, and re-layouts  15 us (4%)
  between operations  14.3 us (4%)
  starting transfers between devices  9.68 us (3%)
  other arithmetic  4.55 us (1%)
    unnamed x9, waiting for transfers between devices  74.4 us
    all_gather x1, waiting for transfers between devices, body(): lax.all_gather(hidden, 'tp', axis=1, tiled=True)  34 us
    all_gather x1, waiting for transfers between devices, body(): lax.all_gather(grad_up_pre, 'tp', axis=1, tiled=True)  33.6 us
    dot_general x3, matrix products, contract_rows(): lax.dot_general(left, right, (((0,), (0,)), ((), ())), preferred_element_...  26.6 us
    psum x1, blocking collectives, body(): grad_combine = lax.psum(local_products, 'tp')  24 us
    all_gather x1, waiting for transfers between devices, body(): piece = lax.all_gather(recv_rows, 'tp', axis=1, tiled=True)  23.8 us
    dot_general x3, matrix products, contract_cols(): lax.dot_general(left, right, (((1,), (1,)), ((), ())), preferred_element_...  19.1 us
    all_to_all x1, blocking collectives, body(): lax.all_to_all(send_grad.reshape(groups, capacity, piece_width), 'ep', sp...  14.8 us
  transfers between devices with their start and end apart: 9, of which 8 were waited for; matrix products, arithmetic and copies ran while one was open for 12% of the time, Pallas kernels for 0%

commit v1 on v0

--- a/solution.py
+++ b/solution.py
@@ -64,7 +64,12 @@
         ),
     )
     recv_rows = recv_rows.reshape(buffer_rows, piece_width)
-    piece = lax.all_gather(recv_rows, "tp", axis=1, tiled=True)
+    ring = [recv_rows]
+    for hop in range(7):
+        ring.append(lax.ppermute(ring[-1], "tp", [(dev, (dev + 1) % 8) for dev in range(8)]))
+    piece = jnp.roll(
+        jnp.concatenate(ring[::-1], axis=1), (lax.axis_index("tp") + 1) * ring[0].shape[1], axis=1
+    )
     gate_pre = jnp.dot(piece, gate_weight, preferred_element_type=jnp.float32)
     up_pre = jnp.dot(piece, up_weight, preferred_element_type=jnp.float32)
     recv_grad = recv_grad.reshape(buffer_rows, piece_width)

time: 346 us -> 344 us (level)
  blocking collectives: 49.5 us -> 38.6 us
  local copies, waits for them, and re-layouts: 15 us -> 18.5 us
    ppermute x0 -> x7, waiting for transfers between devices: none -> 41.6 us  [body(): lax.ppermute(ring[-1], 'tp', [(dev, (dev + 1) % 8) for dev in range(8)])]
    all_gather x1 -> x0, waiting for transfers between devices: 23.8 us -> none  [body(): piece = lax.all_gather(recv_rows, 'tp', axis=1, tiled=True)]
    all_to_all x1 -> x0, blocking collectives: 14.8 us -> none  [body(): lax.all_to_all(send_grad.reshape(groups, capacity, piece_width), 'ep', sp...]
    all_gather x1, waiting for transfers between devices: 14.6 us -> 0.02 us  [body(): lax.all_gather(recv_grad, 'tp', axis=1, tiled=True)]
    all_to_all x1, blocking collectives: 10.8 us -> 14.7 us  [body(): lax.all_to_all(send_rows.reshape(groups, capacity, piece_width), 'ep', sp...]
    unnamed x22 -> x41, local copies, waits for them, and re-layouts: 10.7 us -> 14.1 us
    unnamed x9 -> x8, waiting for transfers between devices: 74.4 us -> 73.6 us
  transfers between devices with their start and end apart: 9 -> 16, of which waited for: 8 -> 14; matrix products, arithmetic and copies ran while one was open for 12% -> 12% of each run, Pallas kernels for 0% -> 0%
where the time goes in v1:
time: 344 us; the launch traced here: 343 us
  waiting for transfers between devices  192 us (56%)
  matrix products  61.2 us (18%)
  blocking collectives  38.6 us (11%)
  local copies, waits for them, and re-layouts  18.5 us (5%)
  between operations  14.4 us (4%)
  starting transfers between devices  13.1 us (4%)
  other arithmetic  4.56 us (1%)
    unnamed x8, waiting for transfers between devices  73.6 us
    ppermute x7, waiting for transfers between devices, body(): lax.ppermute(ring[-1], 'tp', [(dev, (dev + 1) % 8) for dev in range(8)])  41.6 us
    all_gather x1, waiting for transfers between devices, body(): lax.all_gather(hidden, 'tp', axis=1, tiled=True)  34.1 us
    all_gather x1, waiting for transfers between devices, body(): lax.all_gather(grad_up_pre, 'tp', axis=1, tiled=True)  34 us
    dot_general x3, matrix products, contract_rows(): lax.dot_general(left, right, (((0,), (0,)), ((), ())), preferred_element_...  26.6 us
    psum x1, blocking collectives, body(): grad_combine = lax.psum(local_products, 'tp')  24 us
    dot_general x3, matrix products, contract_cols(): lax.dot_general(left, right, (((1,), (1,)), ((), ())), preferred_element_...  19.5 us
    all_to_all x1, blocking collectives, body(): lax.all_to_all(send_rows.reshape(groups, capacity, piece_width), 'ep', sp...  14.7 us
  transfers between devices with their start and end apart: 16, of which 14 were waited for; matrix products, arithmetic and copies ran while one was open for 12% of the time, Pallas kernels for 0%

profile of v1, /device:TPU:0, one launch (start us, length us, event | category | flops | bytes accessed | tf_op | source)
XLA Modules:
  0.0 342.9 jit_solution(13734411588040895843)
XLA Ops:
  7.2 0.8 copy.43
  8.2 1.2 reduce-window.6
  10.0 0.7 multiply_add_fusion.1
  11.1 14.7 %all_to_all.20 = bf16[4,80,384]{2,1,0:T(8,128)(2,1)S(1)} all-to-all(bf16[4,80,384]{2,1,0:T(8,128)(2,1)S(1)} %bitcast.73), channel_id=1, replica_groups=mesh['ep'=4,'tp'=8] {'ep'}, dimensions={0} | all-to-all | bytes 491520 | tf_op jit(solution)/shard_map/all_to_all | solution.py:51
  25.8 1.0 mul.87
  27.0 0.8 copy.42
  27.9 4.4 %collective-permute-done = bf16[320,384]{1,0:T(8,128)(2,1)S(1)} collective-permute-done((bf16[320,384]{1,0:T(8,128)(2,1)S(1)}, bf16[320,384]{1,0:T(8,128)(2,1)S(1)}, u32[]{:S(2)}, u32[]{:S(2)}) %collective-permute-start) | collective-permute-done | bytes 245792 | tf_op jit(solution)/shard_map/ppermute | solution.py:69
  32.3 1.0 convolution_convert_fusion.3
  33.3 3.4 all-to-all-start.2
  36.8 2.0 collective-permute-done.1
  38.8 6.5 %collective-permute-done.2 = bf16[320,384]{1,0:T(8,128)(2,1)S(1)} collective-permute-done((bf16[320,384]{1,0:T(8,128)(2,1)S(1)}, bf16[320,384]{1,0:T(8,128)(2,1)S(1)}, u32[]{:S(2)}, u32[]{:S(2)}) %collective-permute-start.2) | collective-permute-done | bytes 245792 | tf_op jit(solution)/shard_map/ppermute | solution.py:69
  45.3 1.0 all-to-all-done.2
  46.4 0.7 copy-done.2
  47.1 4.7 %collective-permute-done.3 = bf16[320,384]{1,0:T(8,128)(2,1)S(1)} collective-permute-done((bf16[320,384]{1,0:T(8,128)(2,1)S(1)}, bf16[320,384]{1,0:T(8,128)(2,1)S(1)}, u32[]{:S(2)}, u32[]{:S(2)}) %collective-permute-start.3) | collective-permute-done | bytes 245792 | tf_op jit(solution)/shard_map/ppermute | solution.py:69
  51.9 9.2 %collective-permute-done.4 = bf16[320,384]{1,0:T(8,128)(2,1)S(1)} collective-permute-done((bf16[320,384]{1,0:T(8,128)(2,1)S(1)}, bf16[320,384]{1,0:T(8,128)(2,1)S(1)}, u32[]{:S(2)}, u32[]{:S(2)}) %collective-permute-start.4) | collective-permute-done | bytes 245792 | tf_op jit(solution)/shard_map/ppermute | solution.py:69
  61.0 6.6 %collective-permute-done.5 = bf16[320,384]{1,0:T(8,128)(2,1)S(1)} collective-permute-done((bf16[320,384]{1,0:T(8,128)(2,1)S(1)}, bf16[320,384]{1,0:T(8,128)(2,1)S(1)}, u32[]{:S(2)}, u32[]{:S(2)}) %collective-permute-start.5) | collective-permute-done | bytes 245792 | tf_op jit(solution)/shard_map/ppermute | solution.py:69
  67.6 8.2 %collective-permute-done.6 = bf16[320,384]{1,0:T(8,128)(2,1)S(1)} collective-permute-done((bf16[320,384]{1,0:T(8,128)(2,1)S(1)}, bf16[320,384]{1,0:T(8,128)(2,1)S(1)}, u32[]{:S(2)}, u32[]{:S(2)}) %collective-permute-start.6) | collective-permute-done | bytes 245792 | tf_op jit(solution)/shard_map/ppermute | solution.py:69
  76.8 1.9 copy-done.6
  78.7 2.3 fusion.9
  81.0 5.7 %fusion.3 = f32[320,1024]{1,0:T(8,128)S(1)} fusion(bf16[320,3072]{1,0:T(8,128)(2,1)} %all-gather.5.cloned.1.call-done, bf16[1,1024,3072]{2,1,0:T(8,128)(2,1)} %param.15), kind=kOutput, calls=%fused_computation.8 | convolution fusion | flops 2013265920 | bytes 9568256 | tf_op jit(solution)/shard_map/dot_general | solution.py:19
  86.8 6.5 %multiply_convert_fusion.1 = (bf16[320,1024]{1,0:T(8,128)(2,1)}, bf16[320,1024]{1,0:T(8,128)(2,1)S(1)}, bf16[320,1024]{1,0:T(8,128)(2,1)S(1)}) fusion(f32[320,1024]{1,0:T(8,128)S(1)} %fusion.3, f32[320,1024]{1,0:T(8,128)S(1)} %fusion.9, bf16[1,3072,1024]{2,1,0:T(8,128)(2,1)} %param.13, bf16[320,6144]{1,0:T(8,128)(2,1)S(1)} %copy-done.7, s32[]{:T(128)S(6)} %select_n.21), kind=kOutput, calls=%fused_computation.26 | convolution fusion | flops 2018181120 | bytes 12845060 | tf_op jit(solution)/shard_map/dot_general | solution.py:73
  93.3 7.4 %fusion.7 = f32[320,3072]{1,0:T(8,128)} fusion(bf16[320,1024]{1,0:T(8,128)(2,1)S(1)} %get-tuple-element.34, bf16[1,3072,1024]{2,1,0:T(8,128)(2,1)} %param.14), kind=kOutput, calls=%fused_computation.12 | convolution fusion | flops 2013265920 | bytes 10878976 | tf_op jit(solution)/shard_map/dot_general | solution.py:19
  100.7 6.3 %fusion.18 = bf16[320,3072]{1,0:T(8,128)(2,1)S(1)} fusion(f32[320,3072]{1,0:T(8,128)} %fusion.7, bf16[320,1024]{1,0:T(8,128)(2,1)} %get-tuple-element.33, bf16[1,3072,1024]{2,1,0:T(8,128)(2,1)} %param.13), kind=kOutput, calls=%fused_computation.21 | convolution fusion | flops 2015232000 | bytes 12845056 | tf_op jit(solution)/shard_map/dot_general | solution.py:19
  107.1 2.4 copy.51
  109.8 5.0 %fusion.21 = bf16[320,3072]{1,0:T(8,128)(2,1)S(1)} fusion(bf16[320,1024]{1,0:T(8,128)(2,1)S(1)} %get-tuple-element.35, bf16[1,1024,3072]{2,1,0:T(8,128)(2,1)} %param.15), kind=kOutput, calls=%fused_computation.22 | convolution fusion | flops 2014248960 | bytes 8912896 | tf_op jit(solution)/shard_map/dot_general | solution.py:78
  114.8 2.4 copy.49
  117.3 0.5 all-gather.7.cloned.1.call-update
  117.9 0.5 all-gather.9.cloned.1.call-update
  118.5 0.5 all-gather.11.cloned.1.call-update
  119.0 32.1 %reduce-scatter.9.cloned.1.call-done = bf16[384,320]{1,0:T(8,128)(2,1)} async-done(((bf16[3072,320]{1,0:T(8,128)(2,1)}), bf16[384,320]{1,0:T(8,128)(2,1)}) %reduce-scatter.9.cloned.1.call-update) | async-done | bytes 245776
  151.1 1.8 copy.52
  152.9 4.6 %all-to-all-start.3 = ((bf16[4,80,384]{2,1,0:T(8,128)(2,1)}), bf16[4,80,384]{2,1,0:T(8,128)(2,1)S(1)}, u32[]{:S(2)}, u32[]{:S(2)}) async-start(bf16[4,80,384]{2,1,0:T(8,128)(2,1)} %bitcast.11), calls=%async_computation.3 | async-start | bytes 491520 | tf_op jit(solution)/shard_map/all_to_all | solution.py:106
  157.5 39.9 %reduce-scatter.7.cloned.1.call-done = bf16[384,320]{1,0:T(8,128)(2,1)} async-done(((bf16[3072,320]{1,0:T(8,128)(2,1)}), bf16[384,320]{1,0:T(8,128)(2,1)}) %reduce-scatter.7.cloned.1.call-update) | async-done | bytes 245776
  197.4 1.8 copy.50
  199.2 4.6 %all-to-all-start.1 = ((bf16[4,80,384]{2,1,0:T(8,128)(2,1)}), bf16[4,80,384]{2,1,0:T(8,128)(2,1)S(1)}, u32[]{:S(2)}, u32[]{:S(2)}) async-start(bf16[4,80,384]{2,1,0:T(8,128)(2,1)} %bitcast.7), calls=%async_computation.1 | async-start | bytes 491520 | tf_op jit(solution)/shard_map/all_to_all | solution.py:82
  203.8 1.0 gather_fusion.1
  204.8 7.3 %all-to-all-done.1 = bf16[4,80,384]{2,1,0:T(8,128)(2,1)S(1)} async-done(((bf16[4,80,384]{2,1,0:T(8,128)(2,1)}), bf16[4,80,384]{2,1,0:T(8,128)(2,1)S(1)}, u32[]{:S(2)}, u32[]{:S(2)}) %all-to-all-start.1) | async-done | bytes 245792 | tf_op jit(solution)/shard_map/all_to_all | solution.py:82
  212.2 1.0 gather_fusion
  213.9 24.0 %psum.7 = f32[96,2]{1,0:T(8,128)S(1)} all-reduce(f32[96,2]{1,0:T(8,128)S(1)} %reduce_sum.61), channel_id=1, replica_groups=mesh['ep'=4,'tp'=8] {'tp'}, use_global_device_ids=true, to_apply=%region_9.11 | all-reduce | flops 192 | bytes 1536 | tf_op jit(solution)/shard_map/psum | solution.py:96
  237.9 0.6 copy.48
  238.5 1.0 reduce_sum.59
  239.5 1.1 multiply_reduce_fusion.1
  240.6 0.8 all-gather.7.cloned.1.call-done
  241.3 8.7 %fusion = bf16[1,384,8192]{2,1,0:T(8,128)(2,1)} fusion(bf16[320,384]{1,0:T(8,128)(2,1)S(1)} %bitcast.69, bf16[320,8192]{1,0:T(8,128)(2,1)} %all-gather.7.cloned.1.call-done), kind=kOutput, calls=%fused_computation.5 | convolution fusion | flops 2016411648 | bytes 11780096 | tf_op jit(solution)/shard_map/dot_general | solution.py:13
  250.0 34.0 %all-gather.9.cloned.1.call-done = bf16[320,8192]{1,0:T(8,128)(2,1)} async-done(((bf16[320,1024]{1,0:T(8,128)(2,1)}), bf16[320,8192]{1,0:T(8,128)(2,1)}) %all-gather.9.cloned.1.call-update) | async-done | bytes 5242896 | tf_op jit(solution)/shard_map/all_gather | solution.py:126
  284.0 8.7 %fusion.1 = bf16[1,384,8192]{2,1,0:T(8,128)(2,1)} fusion(bf16[320,384]{1,0:T(8,128)(2,1)S(1)} %bitcast.70, bf16[320,8192]{1,0:T(8,128)(2,1)} %all-gather.9.cloned.1.call-done), kind=kOutput, calls=%fused_computation.6 | convolution fusion | flops 2016411648 | bytes 11780096 | tf_op jit(solution)/shard_map/dot_general | solution.py:13
  292.7 34.1 %all-gather.11.cloned.1.call-done = bf16[320,8192]{1,0:T(8,128)(2,1)} async-done(((bf16[320,1024]{1,0:T(8,128)(2,1)}), bf16[320,8192]{1,0:T(8,128)(2,1)}) %all-gather.11.cloned.1.call-update) | async-done | bytes 5242896 | tf_op jit(solution)/shard_map/all_gather | solution.py:120
  326.8 9.3 %fusion.2 = bf16[1,8192,384]{2,1,0:T(8,128)(2,1)} fusion(bf16[320,8192]{1,0:T(8,128)(2,1)} %all-gather.11.cloned.1.call-done, bf16[320,384]{1,0:T(8,128)(2,1)S(1)} %bitcast.72), kind=kOutput, calls=%fused_computation.7 | convolution fusion | flops 2016411648 | bytes 11780096 | tf_op jit(solution)/shard_map/dot_general | solution.py:13
  (76 shorter events, 3.6 us)
Async XLA Ops:
  7.2 3.7 %copy-start = (bf16[96,384]{1,0:T(8,128)(2,1)S(1)}, bf16[96,384]{1,0:T(8,128)(2,1)}, u32[]{:S(2)}) copy-start(bf16[96,384]{1,0:T(8,128)(2,1)} %param.9) | copy-start | bytes 221188
  25.8 6.5 %collective-permute-start = (bf16[320,384]{1,0:T(8,128)(2,1)S(1)}, bf16[320,384]{1,0:T(8,128)(2,1)S(1)}, u32[]{:S(2)}, u32[]{:S(2)}) collective-permute-start(bf16[320,384]{1,0:T(8,128)(2,1)S(1)} %bitcast.66), channel_id=1, source_target_pairs={{0,1},{1,2},{2,3},{3,4},{4,5},{5,6},{6,7},{7,0},{8,9},{9,10},{10,1... | collective-permute-start | bytes 737288 | tf_op jit(solution)/shard_map/ppermute | solution.py:69
  32.3 6.5 %collective-permute-start.1 = (bf16[320,384]{1,0:T(8,128)(2,1)S(1)}, bf16[320,384]{1,0:T(8,128)(2,1)S(1)}, u32[]{:S(2)}, u32[]{:S(2)}) collective-permute-start(bf16[320,384]{1,0:T(8,128)(2,1)S(1)} %collective-permute-done), channel_id=1, source_target_pairs={{0,1},{1,2},{2,3},{3,4},{4,5},{5,6},{6,7},{7,0},{8,9},{9,10},{10,1... | collective-permute-start | bytes 737288 | tf_op jit(solution)/shard_map/ppermute | solution.py:69
  33.3 13.0 %all-to-all-start.2 = ((bf16[4,80,384]{2,1,0:T(8,128)(2,1)}), bf16[4,80,384]{2,1,0:T(8,128)(2,1)S(1)}, u32[]{:S(2)}, u32[]{:S(2)}) async-start(bf16[4,80,384]{2,1,0:T(8,128)(2,1)} %bitcast.9), calls=%async_computation.2 | async-start | bytes 491520 | tf_op jit(solution)/shard_map/all_to_all | solution.py:58
  36.7 44.3 %all-gather.5.cloned.1.call-start = ((), (), s32[]{:S(2)}) async-start(), calls=%async_computation.6 | async-start | bytes 2211840 | tf_op jit(solution)/shard_map/all_gather | solution.py:97
  38.8 6.5 %collective-permute-start.2 = (bf16[320,384]{1,0:T(8,128)(2,1)S(1)}, bf16[320,384]{1,0:T(8,128)(2,1)S(1)}, u32[]{:S(2)}, u32[]{:S(2)}) collective-permute-start(bf16[320,384]{1,0:T(8,128)(2,1)S(1)} %collective-permute-done.1), channel_id=1, source_target_pairs={{0,1},{1,2},{2,3},{3,4},{4,5},{5,6},{6,7},{7,0},{8,9},{9,10},{10,1... | collective-permute-start | bytes 737288 | tf_op jit(solution)/shard_map/ppermute | solution.py:69
  45.3 6.5 %collective-permute-start.3 = (bf16[320,384]{1,0:T(8,128)(2,1)S(1)}, bf16[320,384]{1,0:T(8,128)(2,1)S(1)}, u32[]{:S(2)}, u32[]{:S(2)}) collective-permute-start(bf16[320,384]{1,0:T(8,128)(2,1)S(1)} %collective-permute-done.2), channel_id=1, source_target_pairs={{0,1},{1,2},{2,3},{3,4},{4,5},{5,6},{6,7},{7,0},{8,9},{9,10},{10,1... | collective-permute-start | bytes 737288 | tf_op jit(solution)/shard_map/ppermute | solution.py:69
  46.4 0.7 copy-start.2
  47.1 104.0 %reduce-scatter.9.cloned.1.call-start = ((), (), s32[]{:S(2)}) async-start(), calls=%async_computation.11 | async-start | bytes 2654208
  51.9 9.2 %collective-permute-start.4 = (bf16[320,384]{1,0:T(8,128)(2,1)S(1)}, bf16[320,384]{1,0:T(8,128)(2,1)S(1)}, u32[]{:S(2)}, u32[]{:S(2)}) collective-permute-start(bf16[320,384]{1,0:T(8,128)(2,1)S(1)} %collective-permute-done.3), channel_id=1, source_target_pairs={{0,1},{1,2},{2,3},{3,4},{4,5},{5,6},{6,7},{7,0},{8,9},{9,10},{10,1... | collective-permute-start | bytes 737288 | tf_op jit(solution)/shard_map/ppermute | solution.py:69
  61.0 6.6 %collective-permute-start.5 = (bf16[320,384]{1,0:T(8,128)(2,1)S(1)}, bf16[320,384]{1,0:T(8,128)(2,1)S(1)}, u32[]{:S(2)}, u32[]{:S(2)}) collective-permute-start(bf16[320,384]{1,0:T(8,128)(2,1)S(1)} %collective-permute-done.4), channel_id=1, source_target_pairs={{0,1},{1,2},{2,3},{3,4},{4,5},{5,6},{6,7},{7,0},{8,9},{9,10},{10,1... | collective-permute-start | bytes 737288 | tf_op jit(solution)/shard_map/ppermute | solution.py:69
  67.6 8.2 %collective-permute-start.6 = (bf16[320,384]{1,0:T(8,128)(2,1)S(1)}, bf16[320,384]{1,0:T(8,128)(2,1)S(1)}, u32[]{:S(2)}, u32[]{:S(2)}) collective-permute-start(bf16[320,384]{1,0:T(8,128)(2,1)S(1)} %collective-permute-done.5), channel_id=1, source_target_pairs={{0,1},{1,2},{2,3},{3,4},{4,5},{5,6},{6,7},{7,0},{8,9},{9,10},{10,1... | collective-permute-start | bytes 737288 | tf_op jit(solution)/shard_map/ppermute | solution.py:69
  67.6 11.1 %copy-start.8 = (bf16[1,3072,1024]{2,1,0:T(8,128)(2,1)S(1)}, bf16[1,3072,1024]{2,1,0:T(8,128)(2,1)}, u32[]{:S(2)}) copy-start(bf16[1,3072,1024]{2,1,0:T(8,128)(2,1)} %param.14) | copy-start | bytes 18874372
  76.8 1.9 copy-start.6
  81.0 5.8 %copy-start.7 = (bf16[320,6144]{1,0:T(8,128)(2,1)S(1)}, bf16[320,6144]{1,0:T(8,128)(2,1)}, u32[]{:S(2)}) copy-start(bf16[320,6144]{1,0:T(8,128)(2,1)} %copy-done.6) | copy-start | bytes 11796484
  93.3 7.4 %copy-start.5 = (bf16[320,1024]{1,0:T(8,128)(2,1)}, bf16[320,1024]{1,0:T(8,128)(2,1)S(1)}, u32[]{:S(2)}) copy-start(bf16[320,1024]{1,0:T(8,128)(2,1)S(1)} %get-tuple-element.34) | copy-start | bytes 1966084
  93.3 16.5 %copy-start.4 = (bf16[320,1024]{1,0:T(8,128)(2,1)}, bf16[320,1024]{1,0:T(8,128)(2,1)S(1)}, u32[]{:S(2)}) copy-start(bf16[320,1024]{1,0:T(8,128)(2,1)S(1)} %get-tuple-element.35) | copy-start | bytes 1966084
  109.5 87.9 %reduce-scatter.7.cloned.1.call-start = ((), (), s32[]{:S(2)}) async-start(), calls=%async_computation.10 | async-start | bytes 2654208
  117.3 124.1 %all-gather.7.cloned.1.call-start = ((), (), s32[]{:S(2)}) async-start(), calls=%async_computation.7 | async-start | bytes 5898240 | tf_op jit(solution)/shard_map/all_gather | solution.py:123
  117.9 166.2 %all-gather.9.cloned.1.call-start = ((), (), s32[]{:S(2)}) async-start(), calls=%async_computation.8 | async-start | bytes 5898240 | tf_op jit(solution)/shard_map/all_gather | solution.py:126
  118.4 208.4 %all-gather.11.cloned.1.call-start = ((), (), s32[]{:S(2)}) async-start(), calls=%async_computation.9 | async-start | bytes 5898240 | tf_op jit(solution)/shard_map/all_gather | solution.py:120
  152.9 46.3 %all-to-all-start.3 = ((bf16[4,80,384]{2,1,0:T(8,128)(2,1)}), bf16[4,80,384]{2,1,0:T(8,128)(2,1)S(1)}, u32[]{:S(2)}, u32[]{:S(2)}) async-start(bf16[4,80,384]{2,1,0:T(8,128)(2,1)} %bitcast.11), calls=%async_computation.3 | async-start | bytes 491520 | tf_op jit(solution)/shard_map/all_to_all | solution.py:106
  199.2 12.9 %all-to-all-start.1 = ((bf16[4,80,384]{2,1,0:T(8,128)(2,1)}), bf16[4,80,384]{2,1,0:T(8,128)(2,1)S(1)}, u32[]{:S(2)}, u32[]{:S(2)}) async-start(bf16[4,80,384]{2,1,0:T(8,128)(2,1)} %bitcast.7), calls=%async_computation.1 | async-start | bytes 491520 | tf_op jit(solution)/shard_map/all_to_all | solution.py:82
  250.0 76.8 %copy-start.3 = (bf16[4,80,384]{2,1,0:T(8,128)(2,1)S(1)}, bf16[4,80,384]{2,1,0:T(8,128)(2,1)}, u32[]{:S(2)}) copy-start(bf16[4,80,384]{2,1,0:T(8,128)(2,1)} %copy-done.2) | copy-start | bytes 737284
  284.0 52.0 %copy-start.1 = (bf16[96,384]{1,0:T(8,128)(2,1)S(1)}, bf16[96,384]{1,0:T(8,128)(2,1)}, u32[]{:S(2)}) copy-start(bf16[96,384]{1,0:T(8,128)(2,1)} %param.9) | copy-start | bytes 221188
Sparse Core Ops, SparseCore 0:
  47.2 28.0 all-gather.4
  109.6 41.4 reduce-scatter.8
  155.0 42.3 reduce-scatter.6
  199.7 41.5 all-gather.6
  243.1 40.8 all-gather.8
  285.8 40.9 all-gather.10
